TPU v7x, 32 devices: a whole 2x2x4 slice. The times are simulated.
32 devices in a mesh: wide: 8 (over y, x, core), narrow: 4 (over z).
Axes of the slice: x: 2, y: 2, z: 4, core: 2. Of those that a mesh axis runs over, the one named last changes fastest.
Arguments:
- tokens: bfloat16 [8192, 2048], P(('wide', 'narrow')), may hold values from -6 to 6
- out_grad: bfloat16 [8192, 2048], P(('wide', 'narrow')), may hold values from -6 to 6
- captions: bfloat16 [4096, 4096], P(('wide', 'narrow')), may hold values from -6 to 6
- image_blocks: int32 [32, 256], P('wide'), may hold values from 0 to 3, never falling along the last dimension, each value on 1 to 128 neighbouring positions
- caption_owner: int32 [8, 512], P('wide'), may hold values from 0 to 3, never falling along the last dimension, each value on 1 to 256 neighbouring positions
- norm_gains: float32 [3, 2048], replicated, may hold values from 0.25 to 1.75
- norm_shifts: float32 [3, 2048], replicated, may hold values from -3 to 3
- w_query: float32 [2048, 2048], P('wide', 'narrow'), may hold values from -0.125 to 0.125
- w_key: float32 [2048, 2048], P('wide', 'narrow'), may hold values from -0.125 to 0.125
- w_value: float32 [2048, 2048], P('wide', 'narrow'), may hold values from -0.125 to 0.125
- w_out: float32 [2048, 2048], P('narrow', 'wide'), may hold values from -0.375 to 0.375
- w_cross_query: float32 [2048, 2048], P('wide', 'narrow'), may hold values from -0.125 to 0.125
- w_cross_key: float32 [4096, 2048], P('wide', 'narrow'), may hold values from -0.09375 to 0.09375
- w_cross_value: float32 [4096, 2048], P('wide', 'narrow'), may hold values from -0.09375 to 0.09375
- w_cross_out: float32 [2048, 2048], P('narrow', 'wide'), may hold values from -0.375 to 0.375
- w_up: float32 [2048, 8192], P('wide', 'narrow'), may hold values from -0.125 to 0.125
- w_down: float32 [8192, 2048], P('narrow', 'wide'), may hold values from -0.0625 to 0.0625
Outputs:
- block_out: bfloat16 [8192, 2048], P(('wide', 'narrow'))
- grad_tokens: bfloat16 [8192, 2048], P(('wide', 'narrow'))
- grad_captions: bfloat16 [4096, 4096], P(('wide', 'narrow'))
- grad_norm_gains: float32 [3, 2048], replicated
- grad_norm_shifts: float32 [3, 2048], replicated
- grad_w_query: float32 [2048, 2048], P('wide', 'narrow')
- grad_w_key: float32 [2048, 2048], P('wide', 'narrow')
- grad_w_value: float32 [2048, 2048], P('wide', 'narrow')
- grad_w_out: float32 [2048, 2048], P('narrow', 'wide')
- grad_w_cross_query: float32 [2048, 2048], P('wide', 'narrow')
- grad_w_cross_key: float32 [4096, 2048], P('wide', 'narrow')
- grad_w_cross_value: float32 [4096, 2048], P('wide', 'narrow')
- grad_w_cross_out: float32 [2048, 2048], P('narrow', 'wide')
- grad_w_up: float32 [2048, 8192], P('wide', 'narrow')
- grad_w_down: float32 [8192, 2048], P('narrow', 'wide')
Inputs may be any that keep to these rules, and one draw needn't show every extreme that they name: `image_blocks`: within an image the block numbers never fall; each of the 4 blocks has 1 to 128 tokens, and one block of every image has exactly that many. `caption_owner`: within a group the owners never fall; every image of the group has 1 to 256 caption tokens, and one image of every group has exactly 256.
All inputs are finite; a program needn't handle non-finite values.
Results may differ from a plain program's by a relative error of at most 0.024.
Values may be sent and summed in bfloat16 or wider, within the bound.
A program may use at most 320 MiB of HBM per device.

v0:
```python
import jax
import jax.numpy as jnp
from jax import lax
from jax.sharding import PartitionSpec as P

HEAD_DIM = 128
PIX = 256
CHUNKS = 2
EPSILON = 1e-06
MASKED = -1000000000.0
BF = jnp.bfloat16
F32 = jnp.float32


def product(left_side, right_side):
    return lax.dot_general(
        left_side, right_side, (((left_side.ndim - 1,), (0,)), ((), ())), preferred_element_type=F32
    )


def right_inner(left_side, right_side):
    return lax.dot_general(
        left_side, right_side, (((left_side.ndim - 1,), (1,)), ((), ())), preferred_element_type=F32
    )


def left_inner(left_side, right_side):
    rows = tuple(range(left_side.ndim - 1))
    return lax.dot_general(
        left_side, right_side, ((rows, rows), ((), ())), preferred_element_type=F32
    )


def follow(value, *others):
    if not others:
        return value
    nothing = sum((o[(0,) * o.ndim].astype(F32) for o in others)) * 0.0
    return value + nothing.astype(value.dtype)


def whole(value):
    return lax.optimization_barrier(value)


def after(value, *others):
    return lax.optimization_barrier((value, *others))[0]


def spread(name, rows, gates={}):
    n = lax.axis_size("narrow")
    here = lax.axis_index("narrow")
    with jax.named_scope("spread_" + name):
        up, down = ([rows], [rows])
        for step in range(1, n):
            one, other = (
                follow(up[-1], *gates.get(step, ())),
                follow(down[-1], *gates.get(step, ())),
            )
            up.append(lax.ppermute(one, "narrow", [(k, k + 1) for k in range(step - 1, n - 1)]))
            down.append(lax.ppermute(other, "narrow", [(k, k - 1) for k in range(1, n - step + 1)]))
        parts = [rows] + [jnp.where(here >= s, up[s], down[n - s]) for s in range(1, n)]
        return (jnp.stack(parts), [(up[s], down[s]) for s in range(1, n)])


def sink(name, parts, gates={}, hops=(), until=None):
    n = lax.axis_size("narrow")
    hops = list(hops)
    with jax.named_scope("sink_" + name):
        for step in range(len(hops) + 1, until or n):
            one, other = (parts[step], parts[n - step])
            if hops:
                one = hops[-1][0].astype(F32) + one.astype(F32)
                other = hops[-1][1].astype(F32) + other.astype(F32)
            one, other = (follow(one, *gates.get(step, ())), follow(other, *gates.get(step, ())))
            up = lax.ppermute(one.astype(BF), "narrow", [(k, k + 1) for k in range(step)])
            down = lax.ppermute(
                other.astype(BF), "narrow", [(k, k - 1) for k in range(n - step, n)]
            )
            hops.append((up, down))
        if until:
            return (None, hops)
        return (up.astype(F32) + down.astype(F32) + parts[0].astype(F32), hops)


def norm_stats(features):
    center = features - jnp.mean(features, axis=-1, keepdims=True)
    rstd = lax.rsqrt(jnp.mean(center * center, axis=-1, keepdims=True) + EPSILON)
    return (center * rstd, rstd)


def norm_back(grad, xhat, rstd, gain):
    scaled = grad * gain
    return rstd * (
        scaled
        - jnp.mean(scaled, axis=-1, keepdims=True)
        - xhat * jnp.mean(scaled * xhat, axis=-1, keepdims=True)
    )


def norm_sums(grad, xhat):
    return jnp.stack([jnp.sum(grad * xhat, axis=0), jnp.sum(grad, axis=0)])


def score_block(queries, keys_in, allowed, score_scale):
    raw = jnp.einsum("iphe,iqhe->ihpq", queries, keys_in, preferred_element_type=F32)
    return jnp.where(allowed[:, None], raw * score_scale, MASKED)


def attend(queries, keys_in, values_in, allowed, score_scale):
    scores = score_block(queries, keys_in, allowed, score_scale)
    log_total = jax.nn.logsumexp(scores, axis=-1, keepdims=True)
    soft = jnp.exp(scores - log_total).astype(BF)
    mixture = jnp.einsum("ihpq,iqhe->iphe", soft, values_in, preferred_element_type=F32)
    return (mixture.astype(BF), log_total)


def attend_back(queries, keys_in, values_in, allowed, log_total, grad_mix, score_scale):
    soft = jnp.exp(score_block(queries, keys_in, allowed, score_scale) - log_total)
    grad_soft = jnp.einsum("iphe,iqhe->ihpq", grad_mix, values_in, preferred_element_type=F32)
    grad_values = jnp.einsum(
        "ihpq,iphe->iqhe", whole(soft.astype(BF)), grad_mix, preferred_element_type=F32
    )
    row_dot = jnp.sum(soft * grad_soft, axis=-1, keepdims=True)
    grad_scores = whole((soft * (grad_soft - row_dot) * score_scale).astype(BF))
    grad_queries = jnp.einsum("ihpq,iqhe->iphe", grad_scores, keys_in, preferred_element_type=F32)
    grad_keys = jnp.einsum("ihpq,iphe->iqhe", grad_scores, queries, preferred_element_type=F32)
    return (grad_queries.astype(BF), grad_keys, grad_values)


def body(
    tokens,
    out_grad,
    captions,
    image_blocks,
    caption_owner,
    norm_gains,
    norm_shifts,
    w_query,
    w_key,
    w_value,
    w_out,
    w_cross_query,
    w_cross_key,
    w_cross_value,
    w_cross_out,
    w_up,
    w_down,
):
    scale = HEAD_DIM ** (-0.5)
    n = lax.axis_size("narrow")
    here = lax.axis_index("narrow")
    width = w_query.shape[1]
    heads = width // HEAD_DIM
    part = PIX // CHUNKS
    chunks = [slice(c * part, (c + 1) * part) for c in range(CHUNKS)]
    image_of = (here - jnp.arange(n)) % n

    def rows_of(*pieces):
        return lax.all_gather(
            jnp.concatenate([p.astype(BF) for p in pieces], axis=1), "wide", axis=0, tiled=True
        )

    def columns_of(piece):
        return lax.all_gather(piece.astype(BF), "wide", axis=1, tiled=True)

    def to_rows(g):
        return lax.psum_scatter(g.astype(BF), "wide", scatter_dimension=0, tiled=True).astype(F32)

    def to_columns(g):
        return lax.psum_scatter(g.astype(BF), "wide", scatter_dimension=1, tiled=True).astype(F32)

    full_qkv = rows_of(w_query, w_key, w_value)
    residual0 = tokens.astype(F32)
    xhat1, rstd1 = norm_stats(residual0)
    own1 = (xhat1 * norm_gains[0] + norm_shifts[0]).astype(BF)
    full_out = columns_of(w_out)
    full_ckv = rows_of(w_cross_key, w_cross_value)
    full_cq = rows_of(w_cross_query)
    full_cout = columns_of(w_cross_out)
    full_up = rows_of(w_up)
    full_down = columns_of(w_down)
    normed1 = spread("n1", own1)[0]
    qkv = product(normed1, full_qkv).astype(BF)
    heads_of = lambda x: x.reshape(x.shape[:-1] + (x.shape[-1] // HEAD_DIM, HEAD_DIM))
    self_q, self_k, self_v = [heads_of(qkv[..., k * width : (k + 1) * width]) for k in range(3)]
    blocks = image_blocks[image_of]
    self_allowed = blocks[:, :, None] == blocks[:, None, :]
    self_mix, self_total = attend(self_q, self_k, self_v, self_allowed, scale)
    self_mix = self_mix.reshape(n, PIX, width)
    text = spread("text", follow(captions, normed1[1], normed1[n - 1]), {2: (self_mix,)})[0]
    text_count = text.shape[0] * text.shape[1]
    text_rows = text.reshape(text_count, text.shape[2])
    ckv = product(text_rows, full_ckv).astype(BF)
    cross_k = heads_of(ckv[None, :, :width])
    cross_v = heads_of(ckv[None, :, width:])
    owner = caption_owner[0].reshape(n, -1)[image_of].reshape(-1)
    part_image = jnp.repeat(image_of, part)
    cross_allowed = (part_image[:, None] == owner[None, :])[None]
    state = []
    for c, rows in enumerate(chunks):
        residual1 = (
            residual0[rows] + sink(f"r1_{c}", product(self_mix[:, rows], full_out).astype(BF))[0]
        )
        xhat2, rstd2 = norm_stats(residual1)
        state.append((residual1, xhat2, rstd2))
    normed2 = [
        spread(f"n2_{c}", (s[1] * norm_gains[1] + norm_shifts[1]).astype(BF))[0]
        for c, s in enumerate(state)
    ]
    grad_all, og_hops = spread("og", follow(out_grad, normed2[0][1], normed2[0][n - 1]))
    cross_q, cross_mix, cross_total, state3 = ([], [], [], [])
    for c in range(CHUNKS):
        if c > 0:
            normed2[c] = follow(normed2[c], sent, *og_hops[0])
        q = heads_of(product(normed2[c], full_cq).astype(BF).reshape(1, n * part, width))
        mix, total = attend(q, cross_k, cross_v, cross_allowed, scale)
        mix = mix.reshape(n, part, width)
        sent = whole(product(mix, full_cout).astype(BF))
        residual2 = state[c][0] + sink(f"r2_{c}", sent, {1: og_hops[1]} if c > 0 else {})[0]
        xhat3, rstd3 = norm_stats(residual2)
        cross_q.append(q)
        cross_mix.append(mix)
        cross_total.append(total)
        state3.append((residual2, xhat3, rstd3))
    normed3 = [
        spread(f"n3_{c}", (s[1] * norm_gains[2] + norm_shifts[2]).astype(BF))[0]
        for c, s in enumerate(state3)
    ]
    out_parts, acts, grad_hiddens, grad2, sums3 = ([], [], [], [], [])
    for c, rows in enumerate(chunks):
        hidden = product(normed3[c], full_up)
        grad_rows = grad_all[:, rows]
        acted, gelu_back = jax.vjp(jax.nn.gelu, hidden)
        acted = acted.astype(BF)
        grad_hidden = gelu_back(right_inner(grad_rows, full_down))[0].astype(BF)
        acts.append(acted)
        grad_hiddens.append(grad_hidden)
        grad_n3 = sink(f"d3_{c}", right_inner(grad_hidden, full_up).astype(BF))[0]
        residual2, xhat3, rstd3 = state3[c]
        sums3.append(norm_sums(grad_n3, xhat3))
        grad2.append(out_grad[rows].astype(F32) + norm_back(grad_n3, xhat3, rstd3, norm_gains[2]))
        out_parts.append(whole(product(acted, full_down).astype(BF)))
    cat = lambda xs: jnp.concatenate(xs, axis=1)
    acted, grad_hidden, n3 = (cat(acts), cat(grad_hiddens), cat(normed3))
    grad_down = left_inner(acted, cat([grad_all[:, rows] for rows in chunks]))
    grad_up = left_inner(n3, grad_hidden)
    e2, e2_hops = map(list, zip(*[spread(f"e2_{c}", g.astype(BF)) for c, g in enumerate(grad2)]))
    out_parts = [jnp.concatenate([p[k] for p in out_parts]) for k in range(n)]
    out_hops = sink("out", out_parts, {1: e2_hops[-1][1]}, until=n - 1)[1]
    own_down = to_columns(grad_down)
    own_up = to_rows(grad_up)
    e2[-1] = after(e2[-1], grad_down, grad_up)
    grad1, sums2, grad_cqs, grad_ck, grad_cv = ([], [], [], 0.0, 0.0)
    for c in range(CHUNKS):
        grad_mix = heads_of(right_inner(e2[c], full_cout).astype(BF).reshape(1, n * part, width))
        gq, gk, gv = attend_back(
            cross_q[c], cross_k, cross_v, cross_allowed, cross_total[c], grad_mix, scale
        )
        gq = gq.reshape(n, part, width)
        grad_cqs.append(gq)
        grad_ck = grad_ck + gk
        grad_cv = grad_cv + gv
        sent = whole(right_inner(gq if c == 0 else follow(gq, *out_hops[0]), full_cq).astype(BF))
        grad_n2 = sink(f"d2_{c}", sent, {1: out_hops[1]} if c > 0 else {})[0]
        _, xhat2, rstd2 = state[c]
        sums2.append(norm_sums(grad_n2, xhat2))
        grad1.append(grad2[c] + norm_back(grad_n2, xhat2, rstd2, norm_gains[1]))
    grad_cout = left_inner(cat(cross_mix), cat(e2))
    grad_cq = left_inner(cat(normed2), cat(grad_cqs))
    grad_ckv = jnp.concatenate(
        [grad_ck.reshape(text_count, width), grad_cv.reshape(text_count, width)], axis=1
    ).astype(BF)
    grad_text_part = whole(right_inner(grad_ckv, full_ckv).astype(BF).reshape(n, -1, text.shape[2]))
    grad_wckv = left_inner(text_rows, grad_ckv)
    e1, e1_hops = map(list, zip(*[spread(f"e1_{c}", g.astype(BF)) for c, g in enumerate(grad1)]))
    own_cout = to_columns(grad_cout)
    own_cq = to_rows(grad_cq)
    own_ckv = to_rows(grad_wckv)
    e1[-1] = after(e1[-1], grad_cout, grad_cq, grad_wckv)
    grad_mix = heads_of(cat([right_inner(e, full_out).astype(BF) for e in e1]))
    grad_mix = after(grad_mix, own_down, own_up)
    gq, gk, gv = attend_back(self_q, self_k, self_v, self_allowed, self_total, grad_mix, scale)
    out_sum, out_hops = sink("out", out_parts, {n - 1: e1_hops[-1][1]}, out_hops)
    block_out = (jnp.concatenate([s[0] for s in state3]) + out_sum).astype(BF)
    grad_text, text_hops = sink("text", grad_text_part, {1: e1_hops[-1][1], 2: (gq,)})
    grad_text = grad_text.astype(BF)
    grad_qkv = jnp.concatenate([g.astype(BF).reshape(n, PIX, width) for g in (gq, gk, gv)], axis=-1)
    grad_qkv = follow(grad_qkv, *text_hops[1])
    grad_out = left_inner(self_mix, cat(e1))
    grad_n1_part = whole(right_inner(grad_qkv, full_qkv).astype(BF))
    grad_n1 = sink("d1", grad_n1_part, {1: out_hops[-1]})[0]
    grad_wqkv = left_inner(normed1, after(grad_qkv, grad_n1_part))
    grad1 = jnp.concatenate(grad1)
    grad_n1 = after(grad_n1, own_cout, own_cq, own_ckv)
    grad_tokens = (grad1 + norm_back(grad_n1, xhat1, rstd1, norm_gains[0])).astype(BF)
    sums = lax.psum(
        jnp.stack([norm_sums(grad_n1, xhat1), sum(sums2), sum(sums3)]), ("wide", "narrow")
    )
    own_out = to_columns(grad_out)
    own_qkv = to_rows(grad_wqkv)
    return (
        block_out,
        grad_tokens,
        grad_text,
        sums[:, 0],
        sums[:, 1],
        own_qkv[:, :width],
        own_qkv[:, width : 2 * width],
        own_qkv[:, 2 * width :],
        own_out,
        own_cq,
        own_ckv[:, :width],
        own_ckv[:, width:],
        own_cout,
        own_up,
        own_down,
    )


def solution(mesh):
    in_specs = (
        P(("wide", "narrow"), None),
        P(("wide", "narrow"), None),
        P(("wide", "narrow"), None),
        P("wide", None),
        P("wide", None),
        P(),
        P(),
        P("wide", "narrow"),
        P("wide", "narrow"),
        P("wide", "narrow"),
        P("narrow", "wide"),
        P("wide", "narrow"),
        P("wide", "narrow"),
        P("wide", "narrow"),
        P("narrow", "wide"),
        P("wide", "narrow"),
        P("narrow", "wide"),
    )
    out_specs = (
        P(("wide", "narrow"), None),
        P(("wide", "narrow"), None),
        P(("wide", "narrow"), None),
        P(),
        P(),
        P("wide", "narrow"),
        P("wide", "narrow"),
        P("wide", "narrow"),
        P("narrow", "wide"),
        P("wide", "narrow"),
        P("wide", "narrow"),
        P("wide", "narrow"),
        P("narrow", "wide"),
        P("wide", "narrow"),
        P("narrow", "wide"),
    )
    return jax.shard_map(body, mesh=mesh, in_specs=in_specs, out_specs=out_specs, check_vma=False)
```

profile of v0, /device:TPU:0, one launch (start us, length us, event | category | flops | bytes accessed | tf_op | source)
XLA Modules:
  0.0 1216.4 jit_solution(7606526087314520934)
XLA Ops:
  27.7 21.0 %collective-permute-done = bf16[256,2048]{1,0:T(8,128)(2,1)S(1)} collective-permute-done((bf16[256,2048]{1,0:T(8,128)(2,1)S(1)}, bf16[256,2048]{1,0:T(8,128)(2,1)S(1)}, u32[]{:S(2)}, u32[]{:S(2)}) %collective-permute-start) | collective-permute-done | bytes 1048608 | tf_op jit(solution)/shard_map/spread_n1/ppermute | solution.py:59
  57.3 22.7 %collective-permute-done.2 = bf16[256,2048]{1,0:T(8,128)(2,1)} collective-permute-done((bf16[256,2048]{1,0:T(8,128)(2,1)}, bf16[256,2048]{1,0:T(8,128)(2,1)}, u32[]{:S(2)}, u32[]{:S(2)}) %collective-permute-start.2) | collective-permute-done | bytes 1048608 | tf_op jit(solution)/shard_map/spread_n1/ppermute | solution.py:60
  85.6 19.8 %collective-permute-done.3 = bf16[256,2048]{1,0:T(8,128)(2,1)S(1)} collective-permute-done((bf16[256,2048]{1,0:T(8,128)(2,1)}, bf16[256,2048]{1,0:T(8,128)(2,1)S(1)}, u32[]{:S(2)}, u32[]{:S(2)}) %collective-permute-start.3) | collective-permute-done | bytes 1048608 | tf_op jit(solution)/shard_map/spread_n1/ppermute | solution.py:60
  110.0 10.7 fusion.91
  199.6 11.8 collective-permute-start.12
  212.8 9.2 collective-permute-done.35
  257.6 9.2 collective-permute-done.37
  280.1 9.3 collective-permute-done.38
  352.4 14.3 %collective-permute-start.24 = (bf16[128,2048]{1,0:T(8,128)(2,1)}, bf16[128,2048]{1,0:T(8,128)(2,1)}, u32[]{:S(2)}, u32[]{:S(2)}) collective-permute-start(bf16[128,2048]{1,0:T(8,128)(2,1)} %get-tuple-element.112), channel_id=1, source_target_pairs={{0,1},{4,5},{8,9},{12,13},{16,17},{20,21},{24,25},{28,29}} | collective-permute-start | bytes 1572872 | tf_op jit(solution)/shard_map/sink_r2_0/ppermute | solution.py:75
  396.5 15.2 %collective-permute-start.25 = (bf16[128,2048]{1,0:T(8,128)(2,1)S(1)}, bf16[128,2048]{1,0:T(8,128)(2,1)S(1)}, u32[]{:S(2)}, u32[]{:S(2)}) collective-permute-start(bf16[128,2048]{1,0:T(8,128)(2,1)S(1)} %get-tuple-element.110), channel_id=1, source_target_pairs={{0,1},{1,2},{4,5},{5,6},{8,9},{9,10},{12,13},{13,14},{16,17},{17,1... | collective-permute-start | bytes 1572872 | tf_op jit(solution)/shard_map/sink_r2_0/ppermute | solution.py:75
  497.8 9.2 collective-permute-done.59
  537.7 11.3 multiply_convert_fusion.3
  557.3 11.2 convolution_bitcast_fusion.1
  574.3 10.4 fusion.36
  584.7 9.3 fusion.114
  596.7 11.4 fusion.29
  637.4 11.2 convolution_bitcast_fusion
  704.6 9.3 collective-permute-done.74
  721.1 9.6 collective-permute-done.75
  832.8 10.7 collective-permute-done.77
  971.4 9.7 convolution_convert_fusion
  1051.3 11.4 fusion.94
  1087.3 17.9 %collective-permute-done.124 = bf16[256,2048]{1,0:T(8,128)(2,1)S(1)} collective-permute-done((bf16[256,2048]{1,0:T(8,128)(2,1)S(1)}, bf16[256,2048]{1,0:T(8,128)(2,1)S(1)}, u32[]{:S(2)}, u32[]{:S(2)}) %collective-permute-start.124) | collective-permute-done | bytes 1048608 | tf_op jit(solution)/shard_map/sink_d1/ppermute | solution.py:75
  1163.2 40.0 %psum.7 = f32[3,2,2048]{2,0,1:T(4,128)S(1)} all-reduce(f32[3,2,2048]{2,0,1:T(4,128)S(1)} %pad_maximum_fusion.16), channel_id=1, replica_groups=mesh['wide'=8,'narrow'=4] {'wide','narrow'}, use_global_device_ids=true, to_apply=%region_44.45 | all-reduce | flops 12288 | bytes 98304 | tf_op jit(solution)/shard_map/psum | solution.py:296
  (951 shorter events, 857.0 us)
Async XLA Ops:
  7.2 102.8 %all-gather.8.cloned.1.call-start = ((), (), s32[]{:S(2)}) async-start(), calls=%async_computation.7 | async-start | bytes 7077888 | tf_op jit(solution)/shard_map/all_gather | solution.py:159
  11.6 119.0 %all-gather.10.cloned.1.call-start = ((), (), s32[]{:S(2)}) async-start(), calls=%async_computation.8 | async-start | bytes 2359296 | tf_op jit(solution)/shard_map/all_gather | solution.py:164
  12.4 299.8 %all-gather.14.cloned.1.call-start = ((), (), s32[]{:S(2)}) async-start(), calls=%async_computation.10 | async-start | bytes 2359296 | tf_op jit(solution)/shard_map/all_gather | solution.py:159
  14.4 313.6 %all-gather.12.cloned.1.call-start = ((), (), s32[]{:S(2)}) async-start(), calls=%async_computation.9 | async-start | bytes 9437184 | tf_op jit(solution)/shard_map/all_gather | solution.py:159
  17.0 330.0 %all-gather.16.cloned.1.call-start = ((), (), s32[]{:S(2)}) async-start(), calls=%async_computation.11 | async-start | bytes 2359296 | tf_op jit(solution)/shard_map/all_gather | solution.py:164
  18.8 518.8 %all-gather.18.cloned.1.call-start = ((), (), s32[]{:S(2)}) async-start(), calls=%async_computation.12 | async-start | bytes 9437184 | tf_op jit(solution)/shard_map/all_gather | solution.py:159
  20.0 554.2 %all-gather.20.cloned.1.call-start = ((), (), s32[]{:S(2)}) async-start(), calls=%async_computation.13 | async-start | bytes 9437184 | tf_op jit(solution)/shard_map/all_gather | solution.py:164
  108.5 61.7 %collective-permute-start.13 = (bf16[128,4096]{1,0:T(8,128)(2,1)}, bf16[128,4096]{1,0:T(8,128)(2,1)}, u32[]{:S(2)}, u32[]{:S(2)}) collective-permute-start(bf16[128,4096]{1,0:T(8,128)(2,1)} %broadcast_add_fusion.3), channel_id=1, source_target_pairs={{1,0},{2,1},{3,2},{5,4},{6,5},{7,6},{9,8},{10,9},{11,10},{13,12},{... | collective-permute-start | bytes 3145736 | tf_op jit(solution)/shard_map/spread_text/ppermute | solution.py:60
  150.2 853.7 %reduce-scatter.8.cloned.1.call-start = ((), (), s32[]{:S(2)}) async-start(), calls=%async_computation.14 | async-start | bytes 9437184 | tf_op jit(solution)/shard_map/reduce_scatter | solution.py:170
  301.8 69.0 %collective-permute-start.43 = (bf16[256,2048]{1,0:T(8,128)(2,1)}, bf16[256,2048]{1,0:T(8,128)(2,1)}, u32[]{:S(2)}, u32[]{:S(2)}) collective-permute-start(bf16[256,2048]{1,0:T(8,128)(2,1)} %broadcast_add_fusion), channel_id=1, source_target_pairs={{1,0},{2,1},{3,2},{5,4},{6,5},{7,6},{9,8},{10,9},{11,10},{13,12},{... | collective-permute-start | bytes 3145736 | tf_op jit(solution)/shard_map/spread_og/ppermute | solution.py:60
  303.1 65.2 %collective-permute-start.42 = (bf16[256,2048]{1,0:T(8,128)(2,1)}, bf16[256,2048]{1,0:T(8,128)(2,1)}, u32[]{:S(2)}, u32[]{:S(2)}) collective-permute-start(bf16[256,2048]{1,0:T(8,128)(2,1)} %broadcast_add_fusion), channel_id=1, source_target_pairs={{0,1},{1,2},{2,3},{4,5},{5,6},{6,7},{8,9},{9,10},{10,11},{12,13},{... | collective-permute-start | bytes 3145736 | tf_op jit(solution)/shard_map/spread_og/ppermute | solution.py:59
  432.6 54.0 %collective-permute-start.64 = (bf16[256,2048]{1,0:T(8,128)(2,1)}, bf16[256,2048]{1,0:T(8,128)(2,1)S(1)}, u32[]{:S(2)}, u32[]{:S(2)}) collective-permute-start(bf16[256,2048]{1,0:T(8,128)(2,1)} %collective-permute-done.45), channel_id=1, source_target_pairs={{1,0},{5,4},{9,8},{13,12},{17,16},{21,20},{25,24},{29,28}} | collective-permute-start | bytes 3145736 | tf_op jit(solution)/shard_map/spread_og/ppermute | solution.py:60
  444.0 65.0 %collective-permute-start.65 = (bf16[256,2048]{1,0:T(8,128)(2,1)}, bf16[256,2048]{1,0:T(8,128)(2,1)S(1)}, u32[]{:S(2)}, u32[]{:S(2)}) collective-permute-start(bf16[256,2048]{1,0:T(8,128)(2,1)} %collective-permute-done.44), channel_id=1, source_target_pairs={{2,3},{6,7},{10,11},{14,15},{18,19},{22,23},{26,27},{30,31}} | collective-permute-start | bytes 3145736 | tf_op jit(solution)/shard_map/spread_og/ppermute | solution.py:59
  568.5 438.2 %reduce-scatter.10.cloned.1.call-start = ((), (), s32[]{:S(2)}) async-start(), calls=%async_computation.15 | async-start | bytes 9437184 | tf_op jit(solution)/shard_map/reduce_scatter | solution.py:167
  648.7 434.8 %reduce-scatter.12.cloned.1.call-start = ((), (), s32[]{:S(2)}) async-start(), calls=%async_computation.16 | async-start | bytes 2359296 | tf_op jit(solution)/shard_map/reduce_scatter | solution.py:170
  735.7 78.8 %collective-permute-start.76 = (bf16[256,2048]{1,0:T(8,128)(2,1)}, bf16[256,2048]{1,0:T(8,128)(2,1)}, u32[]{:S(2)}, u32[]{:S(2)}) collective-permute-start(bf16[256,2048]{1,0:T(8,128)(2,1)} %fusion.318), channel_id=1, source_target_pairs={{0,1},{4,5},{8,9},{12,13},{16,17},{20,21},{24,25},{28,29}} | collective-permute-start | bytes 3145736 | tf_op jit(solution)/shard_map/sink_out/ppermute | solution.py:75
  740.5 74.0 %collective-permute-start.80 = (bf16[256,2048]{1,0:T(8,128)(2,1)}, bf16[256,2048]{1,0:T(8,128)(2,1)}, u32[]{:S(2)}, u32[]{:S(2)}) collective-permute-start(bf16[256,2048]{1,0:T(8,128)(2,1)} %fusion.317), channel_id=1, source_target_pairs={{3,2},{7,6},{11,10},{15,14},{19,18},{23,22},{27,26},{31,30}} | collective-permute-start | bytes 3145736 | tf_op jit(solution)/shard_map/sink_out/ppermute | solution.py:76
  788.2 64.2 %collective-permute-start.106 = (bf16[128,2048]{1,0:T(8,128)(2,1)}, bf16[128,2048]{1,0:T(8,128)(2,1)}, u32[]{:S(2)}, u32[]{:S(2)}) collective-permute-start(bf16[128,2048]{1,0:T(8,128)(2,1)} %get-tuple-element.80), channel_id=1, source_target_pairs={{0,1},{4,5},{8,9},{12,13},{16,17},{20,21},{24,25},{28,29}} | collective-permute-start | bytes 1572872 | tf_op jit(solution)/shard_map/sink_d2_0/ppermute | solution.py:75
  790.5 61.9 %collective-permute-start.109 = (bf16[128,2048]{1,0:T(8,128)(2,1)}, bf16[128,2048]{1,0:T(8,128)(2,1)}, u32[]{:S(2)}, u32[]{:S(2)}) collective-permute-start(bf16[128,2048]{1,0:T(8,128)(2,1)} %get-tuple-element.81), channel_id=1, source_target_pairs={{3,2},{7,6},{11,10},{15,14},{19,18},{23,22},{27,26},{31,30}} | collective-permute-start | bytes 1572872 | tf_op jit(solution)/shard_map/sink_d2_0/ppermute | solution.py:76
  814.4 270.9 %reduce-scatter.14.cloned.1.call-start = ((), (), s32[]{:S(2)}) async-start(), calls=%async_computation.17 | async-start | bytes 2359296 | tf_op jit(solution)/shard_map/reduce_scatter | solution.py:167
  880.4 245.2 %reduce-scatter.20.cloned.1.call-start = ((), (), s32[]{:S(2)}) async-start(), calls=%async_computation.20 | async-start | bytes 2359296 | tf_op jit(solution)/shard_map/reduce_scatter | solution.py:170
  970.2 178.2 %reduce-scatter.16.cloned.1.call-start = ((), (), s32[]{:S(2)}) async-start(), calls=%async_computation.18 | async-start | bytes 9437184 | tf_op jit(solution)/shard_map/reduce_scatter | solution.py:167
  970.9 236.3 %reduce-scatter.18.cloned.1.call-start = ((), (), s32[]{:S(2)}) async-start(), calls=%async_computation.19 | async-start | bytes 7077888 | tf_op jit(solution)/shard_map/reduce_scatter | solution.py:167
  987.6 84.0 %collective-permute-start.92 = (bf16[256,2048]{1,0:T(8,128)(2,1)}, bf16[256,2048]{1,0:T(8,128)(2,1)}, u32[]{:S(2)}, u32[]{:S(2)}) collective-permute-start(bf16[256,2048]{1,0:T(8,128)(2,1)} %add_convert_fusion.1), channel_id=1, source_target_pairs={{0,1},{1,2},{2,3},{4,5},{5,6},{6,7},{8,9},{9,10},{10,11},{12,13},{... | collective-permute-start | bytes 3145736 | tf_op jit(solution)/shard_map/sink_out/ppermute | solution.py:75
  (319 other events, 6870.8 us)
Sparse Core Ops, SparseCore 0:
  11.7 48.1 all-gather.7
  62.3 28.0 all-gather.9
  92.9 27.7 all-gather.13
  122.4 54.2 all-gather.11
  178.4 28.0 all-gather.15
  208.3 54.2 all-gather.17
  264.5 55.8 all-gather.19
  568.6 74.8 reduce-scatter.7
  648.8 76.2 reduce-scatter.9
  814.5 40.9 reduce-scatter.11
  880.5 42.3 reduce-scatter.13
  970.3 40.5 reduce-scatter.19
  1014.3 71.4 reduce-scatter.15
  1089.0 61.7 reduce-scatter.17
where the time goes:
time: 1230 us; the launch traced here: 1220 us
  starting transfers between devices  335 us (27%)
  waiting for transfers between devices  309 us (25%)
  matrix products  250 us (20%)
  other arithmetic  162 us (13%)
  local copies, waits for them, and re-layouts  86.3 us (7%)
  blocking collectives  40 us (3%)
  between operations  33.3 us (3%)
    ppermute x33, waiting for transfers between devices, spread(): lax.ppermute(other, 'narrow', [(k, k - 1) for k in range(1, n - step + 1)])  169 us
    ppermute x33, starting transfers between devices, sink(): lax.ppermute(one.astype(BF), 'narrow', [(k, k + 1) for k in range(step)])  158 us
    ppermute x33, starting transfers between devices, spread(): lax.ppermute(one, 'narrow', [(k, k + 1) for k in range(step - 1, n - 1)])  89.9 us
    ppermute x33, waiting for transfers between devices, sink(): lax.ppermute(one.astype(BF), 'narrow', [(k, k + 1) for k in range(step)])  81.6 us
    dot_general x12, matrix products, right_inner(): lax.dot_general(left_side, right_side, (((left_side.ndim - 1,), (1,)), ((...  72.9 us
    dot_general x12, matrix products, product(): lax.dot_general(left_side, right_side, (((left_side.ndim - 1,), (0,)), ((...  68.6 us
    dot_general x7, matrix products, left_inner(): lax.dot_general(left_side, right_side, ((rows, rows), ((), ())), preferre...  52.4 us
    ppermute x33, starting transfers between devices, spread(): lax.ppermute(other, 'narrow', [(k, k - 1) for k in range(1, n - step + 1)])  43.1 us
  transfers between devices with their start and end apart: 146, of which 46 were waited for; matrix products, arithmetic and copies ran while one was open for 39% of the time, Pallas kernels for 0%

commit v1 on v0

--- a/solution.py
+++ b/solution.py
@@ -1,3 +1,4 @@
+import functools
 import jax
 import jax.numpy as jnp
 from jax import lax
@@ -10,6 +11,13 @@
 MASKED = -1000000000.0
 BF = jnp.bfloat16
 F32 = jnp.float32
+
+
+def match_packet(row_data, dev_axis):
+    return jnp.sum(lax.all_gather(row_data, axis_name=dev_axis), axis=0)
+
+
+joints_number = functools.partial(match_packet, dev_axis=("wide", "narrow"))
 
 
 def product(left_side, right_side):
@@ -293,9 +301,7 @@
     grad1 = jnp.concatenate(grad1)
     grad_n1 = after(grad_n1, own_cout, own_cq, own_ckv)
     grad_tokens = (grad1 + norm_back(grad_n1, xhat1, rstd1, norm_gains[0])).astype(BF)
-    sums = lax.psum(
-        jnp.stack([norm_sums(grad_n1, xhat1), sum(sums2), sum(sums3)]), ("wide", "narrow")
-    )
+    sums = joints_number(jnp.stack([norm_sums(grad_n1, xhat1), sum(sums2), sum(sums3)]))
     own_out = to_columns(grad_out)
     own_qkv = to_rows(grad_wqkv)
     return (

time: 1230 us -> 1280 us (1.041)
  waiting for transfers between devices: 309 us -> 396 us
  blocking collectives: 40 us -> 0 us
    reduce_scatter x4, waiting for transfers between devices: 0.03 us -> 60.6 us  [to_rows(): lax.psum_scatter(g.astype(BF), 'wide', scatter_dimension=0, tiled=True)]
    psum x1 -> x0, blocking collectives: 40 us -> none  [body(): lax.psum(jnp.stack([norm_sums(grad_n1, xhat1), sum(sums2), sum(sums3)]),...]
    ppermute x33, waiting for transfers between devices: 81.6 us -> 95.2 us  [sink(): lax.ppermute(one.astype(BF), 'narrow', [(k, k + 1) for k in range(step)])]
  transfers between devices with their start and end apart: 146 -> 147, of which waited for: 46 -> 47; matrix products, arithmetic and copies ran while one was open for 39% -> 37% of each run, Pallas kernels for 0% -> 0%
where the time goes in v1:
time: 1280 us; the launch traced here: 1270 us
  waiting for transfers between devices  396 us (31%)
  starting transfers between devices  344 us (27%)
  matrix products  251 us (20%)
  other arithmetic  161 us (13%)
  local copies, waits for them, and re-layouts  86.9 us (7%)
  between operations  33.5 us (3%)
    ppermute x33, waiting for transfers between devices, spread(): lax.ppermute(other, 'narrow', [(k, k - 1) for k in range(1, n - step + 1)])  169 us
    ppermute x33, starting transfers between devices, sink(): lax.ppermute(one.astype(BF), 'narrow', [(k, k + 1) for k in range(step)])  166 us
    ppermute x33, waiting for transfers between devices, sink(): lax.ppermute(one.astype(BF), 'narrow', [(k, k + 1) for k in range(step)])  95.2 us
    ppermute x33, starting transfers between devices, spread(): lax.ppermute(one, 'narrow', [(k, k + 1) for k in range(step - 1, n - 1)])  91.7 us
    dot_general x12, matrix products, right_inner(): lax.dot_general(left_side, right_side, (((left_side.ndim - 1,), (1,)), ((...  69.6 us
    dot_general x12, matrix products, product(): lax.dot_general(left_side, right_side, (((left_side.ndim - 1,), (0,)), ((...  68.5 us
    reduce_scatter x4, waiting for transfers between devices, to_rows(): lax.psum_scatter(g.astype(BF), 'wide', scatter_dimension=0, tiled=True)  60.6 us
    dot_general x7, matrix products, left_inner(): lax.dot_general(left_side, right_side, ((rows, rows), ((), ())), preferre...  55.1 us
  transfers between devices with their start and end apart: 147, of which 47 were waited for; matrix products, arithmetic and copies ran while one was open for 37% of the time, Pallas kernels for 0%

profile of v1, /device:TPU:0, one launch (start us, length us, event | category | flops | bytes accessed | tf_op | source)
XLA Modules:
  0.0 1273.4 jit_solution(61746306979616526)
XLA Ops:
  27.7 21.0 %collective-permute-done = bf16[256,2048]{1,0:T(8,128)(2,1)S(1)} collective-permute-done((bf16[256,2048]{1,0:T(8,128)(2,1)S(1)}, bf16[256,2048]{1,0:T(8,128)(2,1)S(1)}, u32[]{:S(2)}, u32[]{:S(2)}) %collective-permute-start) | collective-permute-done | bytes 1048608 | tf_op jit(solution)/shard_map/spread_n1/ppermute | solution.py:67
  57.3 22.7 %collective-permute-done.2 = bf16[256,2048]{1,0:T(8,128)(2,1)} collective-permute-done((bf16[256,2048]{1,0:T(8,128)(2,1)}, bf16[256,2048]{1,0:T(8,128)(2,1)}, u32[]{:S(2)}, u32[]{:S(2)}) %collective-permute-start.2) | collective-permute-done | bytes 1048608 | tf_op jit(solution)/shard_map/spread_n1/ppermute | solution.py:68
  85.6 19.8 %collective-permute-done.3 = bf16[256,2048]{1,0:T(8,128)(2,1)S(1)} collective-permute-done((bf16[256,2048]{1,0:T(8,128)(2,1)}, bf16[256,2048]{1,0:T(8,128)(2,1)S(1)}, u32[]{:S(2)}, u32[]{:S(2)}) %collective-permute-start.3) | collective-permute-done | bytes 1048608 | tf_op jit(solution)/shard_map/spread_n1/ppermute | solution.py:68
  110.1 10.7 fusion.91
  199.7 11.8 collective-permute-start.12
  280.1 9.3 collective-permute-done.38
  352.5 14.3 %collective-permute-start.24 = (bf16[128,2048]{1,0:T(8,128)(2,1)}, bf16[128,2048]{1,0:T(8,128)(2,1)}, u32[]{:S(2)}, u32[]{:S(2)}) collective-permute-start(bf16[128,2048]{1,0:T(8,128)(2,1)} %get-tuple-element.112), channel_id=1, source_target_pairs={{0,1},{4,5},{8,9},{12,13},{16,17},{20,21},{24,25},{28,29}} | collective-permute-start | bytes 1572872 | tf_op jit(solution)/shard_map/sink_r2_0/ppermute | solution.py:83
  396.6 15.2 %collective-permute-start.25 = (bf16[128,2048]{1,0:T(8,128)(2,1)S(1)}, bf16[128,2048]{1,0:T(8,128)(2,1)S(1)}, u32[]{:S(2)}, u32[]{:S(2)}) collective-permute-start(bf16[128,2048]{1,0:T(8,128)(2,1)S(1)} %get-tuple-element.110), channel_id=1, source_target_pairs={{0,1},{1,2},{4,5},{5,6},{8,9},{9,10},{12,13},{13,14},{16,17},{17,1... | collective-permute-start | bytes 1572872 | tf_op jit(solution)/shard_map/sink_r2_0/ppermute | solution.py:83
  537.8 11.4 multiply_convert_fusion.3
  557.3 11.2 convolution_bitcast_fusion.1
  574.3 10.4 fusion.36
  584.8 9.3 fusion.114
  596.8 11.4 fusion.29
  637.4 11.2 convolution_bitcast_fusion
  704.2 9.5 collective-permute-done.74
  720.9 9.6 collective-permute-done.75
  934.1 9.6 convolution_convert_fusion
  953.5 12.0 collective-permute-start.92
  977.0 15.1 %collective-permute-done.118 = bf16[128,2048]{1,0:T(8,128)(2,1)S(1)} collective-permute-done((bf16[128,2048]{1,0:T(8,128)(2,1)}, bf16[128,2048]{1,0:T(8,128)(2,1)S(1)}, u32[]{:S(2)}, u32[]{:S(2)}) %collective-permute-start.118) | collective-permute-done | bytes 524320 | tf_op jit(solution)/shard_map/spread_e1_1/ppermute | solution.py:68
  1060.8 10.0 fusion.94
  1076.7 14.1 %collective-permute-done.124 = bf16[256,2048]{1,0:T(8,128)(2,1)S(1)} collective-permute-done((bf16[256,2048]{1,0:T(8,128)(2,1)S(1)}, bf16[256,2048]{1,0:T(8,128)(2,1)S(1)}, u32[]{:S(2)}, u32[]{:S(2)}) %collective-permute-start.124) | collective-permute-done | bytes 1048608 | tf_op jit(solution)/shard_map/sink_d1/ppermute | solution.py:83
  1101.2 13.5 %collective-permute-done.125 = bf16[256,2048]{1,0:T(8,128)(2,1)S(1)} collective-permute-done((bf16[256,2048]{1,0:T(8,128)(2,1)S(1)}, bf16[256,2048]{1,0:T(8,128)(2,1)S(1)}, u32[]{:S(2)}, u32[]{:S(2)}) %collective-permute-start.125) | collective-permute-done | bytes 1048608 | tf_op jit(solution)/shard_map/sink_d1/ppermute | solution.py:83
  1146.2 11.5 bitcast_convert_fusion
  1203.5 60.5 %reduce-scatter.18.cloned.1.call-done = bf16[256,1536]{1,0:T(8,128)(2,1)} async-done(((bf16[2048,1536]{1,0:T(8,128)(2,1)}), bf16[256,1536]{1,0:T(8,128)(2,1)}) %reduce-scatter.18.cloned.1.call-update) | async-done | bytes 786448 | tf_op jit(solution)/shard_map/reduce_scatter | solution.py:175
  (937 shorter events, 884.8 us)
Async XLA Ops:
  7.2 102.8 %all-gather.10.cloned.1.call-start = ((), (), s32[]{:S(2)}) async-start(), calls=%async_computation.7 | async-start | bytes 7077888 | tf_op jit(solution)/shard_map/all_gather | solution.py:167
  11.6 119.0 %all-gather.12.cloned.1.call-start = ((), (), s32[]{:S(2)}) async-start(), calls=%async_computation.8 | async-start | bytes 2359296 | tf_op jit(solution)/shard_map/all_gather | solution.py:172
  12.4 299.8 %all-gather.16.cloned.1.call-start = ((), (), s32[]{:S(2)}) async-start(), calls=%async_computation.10 | async-start | bytes 2359296 | tf_op jit(solution)/shard_map/all_gather | solution.py:167
  14.4 313.7 %all-gather.14.cloned.1.call-start = ((), (), s32[]{:S(2)}) async-start(), calls=%async_computation.9 | async-start | bytes 9437184 | tf_op jit(solution)/shard_map/all_gather | solution.py:167
  17.0 330.0 %all-gather.18.cloned.1.call-start = ((), (), s32[]{:S(2)}) async-start(), calls=%async_computation.11 | async-start | bytes 2359296 | tf_op jit(solution)/shard_map/all_gather | solution.py:172
  18.8 518.9 %all-gather.20.cloned.1.call-start = ((), (), s32[]{:S(2)}) async-start(), calls=%async_computation.12 | async-start | bytes 9437184 | tf_op jit(solution)/shard_map/all_gather | solution.py:167
  20.0 554.3 %all-gather.22.cloned.1.call-start = ((), (), s32[]{:S(2)}) async-start(), calls=%async_computation.13 | async-start | bytes 9437184 | tf_op jit(solution)/shard_map/all_gather | solution.py:172
  150.2 859.6 %reduce-scatter.8.cloned.1.call-start = ((), (), s32[]{:S(2)}) async-start(), calls=%async_computation.14 | async-start | bytes 9437184 | tf_op jit(solution)/shard_map/reduce_scatter | solution.py:178
  301.8 69.1 %collective-permute-start.43 = (bf16[256,2048]{1,0:T(8,128)(2,1)}, bf16[256,2048]{1,0:T(8,128)(2,1)}, u32[]{:S(2)}, u32[]{:S(2)}) collective-permute-start(bf16[256,2048]{1,0:T(8,128)(2,1)} %broadcast_add_fusion), channel_id=1, source_target_pairs={{1,0},{2,1},{3,2},{5,4},{6,5},{7,6},{9,8},{10,9},{11,10},{13,12},{... | collective-permute-start | bytes 3145736 | tf_op jit(solution)/shard_map/spread_og/ppermute | solution.py:68
  303.1 65.3 %collective-permute-start.42 = (bf16[256,2048]{1,0:T(8,128)(2,1)}, bf16[256,2048]{1,0:T(8,128)(2,1)}, u32[]{:S(2)}, u32[]{:S(2)}) collective-permute-start(bf16[256,2048]{1,0:T(8,128)(2,1)} %broadcast_add_fusion), channel_id=1, source_target_pairs={{0,1},{1,2},{2,3},{4,5},{5,6},{6,7},{8,9},{9,10},{10,11},{12,13},{... | collective-permute-start | bytes 3145736 | tf_op jit(solution)/shard_map/spread_og/ppermute | solution.py:67
  444.1 65.0 %collective-permute-start.65 = (bf16[256,2048]{1,0:T(8,128)(2,1)}, bf16[256,2048]{1,0:T(8,128)(2,1)S(1)}, u32[]{:S(2)}, u32[]{:S(2)}) collective-permute-start(bf16[256,2048]{1,0:T(8,128)(2,1)} %collective-permute-done.44), channel_id=1, source_target_pairs={{2,3},{6,7},{10,11},{14,15},{18,19},{22,23},{26,27},{30,31}} | collective-permute-start | bytes 3145736 | tf_op jit(solution)/shard_map/spread_og/ppermute | solution.py:67
  568.6 443.9 %reduce-scatter.10.cloned.1.call-start = ((), (), s32[]{:S(2)}) async-start(), calls=%async_computation.15 | async-start | bytes 9437184 | tf_op jit(solution)/shard_map/reduce_scatter | solution.py:175
  648.6 477.9 %reduce-scatter.12.cloned.1.call-start = ((), (), s32[]{:S(2)}) async-start(), calls=%async_computation.16 | async-start | bytes 2359296 | tf_op jit(solution)/shard_map/reduce_scatter | solution.py:178
  735.5 79.1 %collective-permute-start.76 = (bf16[256,2048]{1,0:T(8,128)(2,1)}, bf16[256,2048]{1,0:T(8,128)(2,1)}, u32[]{:S(2)}, u32[]{:S(2)}) collective-permute-start(bf16[256,2048]{1,0:T(8,128)(2,1)} %fusion.318), channel_id=1, source_target_pairs={{0,1},{4,5},{8,9},{12,13},{16,17},{20,21},{24,25},{28,29}} | collective-permute-start | bytes 3145736 | tf_op jit(solution)/shard_map/sink_out/ppermute | solution.py:83
  740.4 74.2 %collective-permute-start.80 = (bf16[256,2048]{1,0:T(8,128)(2,1)}, bf16[256,2048]{1,0:T(8,128)(2,1)}, u32[]{:S(2)}, u32[]{:S(2)}) collective-permute-start(bf16[256,2048]{1,0:T(8,128)(2,1)} %fusion.317), channel_id=1, source_target_pairs={{3,2},{7,6},{11,10},{15,14},{19,18},{23,22},{27,26},{31,30}} | collective-permute-start | bytes 3145736 | tf_op jit(solution)/shard_map/sink_out/ppermute | solution.py:84
  788.2 64.3 %collective-permute-start.106 = (bf16[128,2048]{1,0:T(8,128)(2,1)}, bf16[128,2048]{1,0:T(8,128)(2,1)}, u32[]{:S(2)}, u32[]{:S(2)}) collective-permute-start(bf16[128,2048]{1,0:T(8,128)(2,1)} %get-tuple-element.80), channel_id=1, source_target_pairs={{0,1},{4,5},{8,9},{12,13},{16,17},{20,21},{24,25},{28,29}} | collective-permute-start | bytes 1572872 | tf_op jit(solution)/shard_map/sink_d2_0/ppermute | solution.py:83
  790.4 62.0 %collective-permute-start.109 = (bf16[128,2048]{1,0:T(8,128)(2,1)}, bf16[128,2048]{1,0:T(8,128)(2,1)}, u32[]{:S(2)}, u32[]{:S(2)}) collective-permute-start(bf16[128,2048]{1,0:T(8,128)(2,1)} %get-tuple-element.81), channel_id=1, source_target_pairs={{3,2},{7,6},{11,10},{15,14},{19,18},{23,22},{27,26},{31,30}} | collective-permute-start | bytes 1572872 | tf_op jit(solution)/shard_map/sink_d2_0/ppermute | solution.py:84
  826.2 302.1 %reduce-scatter.14.cloned.1.call-start = ((), (), s32[]{:S(2)}) async-start(), calls=%async_computation.17 | async-start | bytes 2359296 | tf_op jit(solution)/shard_map/reduce_scatter | solution.py:175
  881.6 262.7 %reduce-scatter.16.cloned.1.call-start = ((), (), s32[]{:S(2)}) async-start(), calls=%async_computation.18 | async-start | bytes 9437184 | tf_op jit(solution)/shard_map/reduce_scatter | solution.py:175
  943.8 226.6 %reduce-scatter.20.cloned.1.call-start = ((), (), s32[]{:S(2)}) async-start(), calls=%async_computation.20 | async-start | bytes 2359296 | tf_op jit(solution)/shard_map/reduce_scatter | solution.py:178
  953.5 87.1 %collective-permute-start.92 = (bf16[256,2048]{1,0:T(8,128)(2,1)}, bf16[256,2048]{1,0:T(8,128)(2,1)}, u32[]{:S(2)}, u32[]{:S(2)}) collective-permute-start(bf16[256,2048]{1,0:T(8,128)(2,1)} %add_convert_fusion.1), channel_id=1, source_target_pairs={{0,1},{1,2},{2,3},{4,5},{5,6},{6,7},{8,9},{9,10},{10,11},{12,13},{... | collective-permute-start | bytes 3145736 | tf_op jit(solution)/shard_map/sink_out/ppermute | solution.py:83
  968.2 73.6 %collective-permute-start.93 = (bf16[256,2048]{1,0:T(8,128)(2,1)}, bf16[256,2048]{1,0:T(8,128)(2,1)}, u32[]{:S(2)}, u32[]{:S(2)}) collective-permute-start(bf16[256,2048]{1,0:T(8,128)(2,1)} %add_convert_fusion), channel_id=1, source_target_pairs={{1,0},{2,1},{3,2},{5,4},{6,5},{7,6},{9,8},{10,9},{11,10},{13,12},{... | collective-permute-start | bytes 3145736 | tf_op jit(solution)/shard_map/sink_out/ppermute | solution.py:84
  1101.2 99.0 %all-gather.24.cloned.1.call-start = ((), (), s32[]{:S(2)}) async-start(), calls=%async_computation.21 | async-start | bytes 1622016 | tf_op jit(solution)/shard_map/all_gather | solution.py:17
  1146.2 117.9 %reduce-scatter.18.cloned.1.call-start = ((), (), s32[]{:S(2)}) async-start(), calls=%async_computation.19 | async-start | bytes 7077888 | tf_op jit(solution)/shard_map/reduce_scatter | solution.py:175
  (311 other events, 7027.7 us)
Sparse Core Ops, SparseCore 0:
  11.7 48.1 all-gather.9
  62.3 28.0 all-gather.11
  92.9 27.7 all-gather.15
  122.4 54.2 all-gather.13
  178.4 28.0 all-gather.17
  208.3 54.2 all-gather.19
  264.5 55.8 all-gather.21
  568.7 74.8 reduce-scatter.7
  648.7 76.2 reduce-scatter.9
  826.3 40.8 reduce-scatter.11
  881.8 44.3 reduce-scatter.13
  943.9 73.6 reduce-scatter.15
  1101.3 40.2 reduce-scatter.19
  1146.3 53.8 all-gather.23
  1203.4 60.6 reduce-scatter.17
